TPU v7x, 32 devices: a whole 2x2x4 slice. The times are simulated.
32 devices in a mesh: dp: 8 (over y, x, core), tensor: 4 (over z).
Axes of the slice: x: 2, y: 2, z: 4, core: 2. Of those that a mesh axis runs over, the one named last changes fastest.
Arguments:
- tokens: bfloat16 [32, 256, 1152], P(('dp', 'tensor')), may hold values from -6 to 6
- timesteps: int32 [32], P('dp'), may hold values from 0 to 999
- labels: int32 [32], P('dp'), may hold values from 0 to 999
- item_counts: int32 [8], P('dp'), may hold values from 1 to 4
- cotangent: bfloat16 [32, 256, 1152], P(('dp', 'tensor')), may hold values from -6 to 6
- project_weight: bfloat16 [1152, 3, 1152], P(None, None, 'tensor'), may hold values from -0.1875 to 0.1875
- query_gain: bfloat16 [72], replicated, may hold values from 0.099609375 to 1.8984375
- key_gain: bfloat16 [72], replicated, may hold values from 0.099609375 to 1.8984375
- output_weight: bfloat16 [1152, 1152], P('tensor'), may hold values from -0.5 to 0.5
- output_bias: bfloat16 [1152], replicated, may hold values from -3 to 3
- expand_weight: bfloat16 [1152, 2, 3072], P(None, None, 'tensor'), may hold values from -0.1875 to 0.1875
- down_weight: bfloat16 [3072, 1152], P('tensor'), may hold values from -0.15625 to 0.15625
- down_bias: bfloat16 [1152], replicated, may hold values from -3 to 3
- modulate_weight: bfloat16 [1152, 6, 1152], P(None, None, 'tensor'), may hold values from -0.1875 to 0.1875
- modulate_bias: bfloat16 [6, 1152], P(None, 'tensor'), may hold values from -3 to 3
- time_weight: bfloat16 [256, 1152], replicated, may hold values from -0.5 to 0.5
- time_bias: bfloat16 [1152], replicated, may hold values from -3 to 3
- embed_weight: bfloat16 [1152, 1152], replicated, may hold values from -0.25 to 0.25
- embed_bias: bfloat16 [1152], replicated, may hold values from -3 to 3
- class_table: bfloat16 [1000, 1152], replicated, may hold values from -6 to 6
Outputs:
- result: bfloat16 [32, 256, 1152], P(('dp', 'tensor'))
- tokens_grad: bfloat16 [32, 256, 1152], P(('dp', 'tensor'))
- project_grad: float32 [1152, 3, 1152], P('dp', None, 'tensor')
- query_gain_grad: float32 [72], replicated
- key_gain_grad: float32 [72], replicated
- output_weight_grad: float32 [1152, 1152], P('tensor', 'dp')
- output_bias_grad: float32 [1152], replicated
- expand_grad: float32 [1152, 2, 3072], P('dp', None, 'tensor')
- down_grad: float32 [3072, 1152], P('tensor', 'dp')
- down_bias_grad: float32 [1152], replicated
- modulate_grad: float32 [1152, 6, 1152], P('dp', None, 'tensor')
- modulate_bias_grad: float32 [6, 1152], replicated
- time_grad: float32 [256, 1152], P(None, 'dp')
- time_bias_grad: float32 [1152], P('dp')
- embed_grad: float32 [1152, 1152], P('dp')
- embed_bias_grad: float32 [1152], P('dp')
- class_grad: float32 [1000, 1152], P(None, 'dp')
Inputs may be any that keep to these rules, and one draw needn't show every extreme that they name: `item_counts`: entry i counts the real items among the 4 items of index i of dp; they are its first ones.
All inputs are finite; a program needn't handle non-finite values.
Results may differ from a plain program's by a relative error of at most 0.03.
Values may be sent and summed in bfloat16 or wider, within the bound.
A program may use at most 256 MiB of HBM per device.

v0:
```python
import math
import jax
import jax.numpy as jnp
from jax import lax
from jax.sharding import PartitionSpec as P

HD = 72
FREQ = 256
GRID = 16
EPS = 1e-06


def layer_norm(value):
    center = value - jnp.mean(value, axis=-1, keepdims=True)
    inverse = lax.rsqrt(jnp.mean(center * center, axis=-1, keepdims=True) + EPS)
    return (center * inverse, inverse)


def layer_norm_back(normed, inverse, grad):
    return inverse * (
        grad
        - jnp.mean(grad, axis=-1, keepdims=True)
        - normed * jnp.mean(grad * normed, axis=-1, keepdims=True)
    )


def silu_slope(value):
    sigma = jax.nn.sigmoid(value)
    return sigma * (1.0 + value * (1.0 - sigma))


def rotate(value, positions):
    quarter = HD // 4
    rates = 10000.0 ** (-jnp.arange(quarter, dtype=jnp.float32) / quarter)
    places = ((positions // GRID).astype(jnp.float32), (positions % GRID).astype(jnp.float32))
    pieces = []
    for which_half in range(2):
        half_value = value[..., which_half * 2 * quarter : (which_half + 1) * 2 * quarter]
        angle = places[which_half][:, None] * rates[None, :]
        cosine = jnp.cos(angle)[None, :, None, :]
        sine = jnp.sin(angle)[None, :, None, :]
        first = half_value[..., :quarter]
        second = half_value[..., quarter:]
        pieces.append(first * cosine - second * sine)
        pieces.append(second * cosine + first * sine)
    return jnp.concatenate(pieces, axis=-1)


def head_prepare(raw, gain, positions):
    scaled = raw * lax.rsqrt(jnp.mean(raw * raw, axis=-1, keepdims=True) + EPS) * gain
    return rotate(scaled, positions)


def time_features(steps_in):
    half = FREQ // 2
    rates = jnp.exp(-math.log(10000.0) * jnp.arange(half, dtype=jnp.float32) / half)
    angle = steps_in.astype(jnp.float32)[:, None] * rates[None, :]
    return jnp.concatenate([jnp.cos(angle), jnp.sin(angle)], axis=-1)


def shards(
    tokens,
    timesteps,
    labels,
    item_counts,
    cotangent,
    project_weight,
    query_gain,
    key_gain,
    output_weight,
    output_bias,
    expand_weight,
    down_weight,
    down_bias,
    modulate_weight,
    modulate_bias,
    time_weight,
    time_bias,
    embed_weight,
    embed_bias,
    class_table,
):
    local_items, length, width = tokens.shape
    items = timesteps.shape[0]
    slab = modulate_weight.shape[2]
    heads_here = project_weight.shape[2] // HD
    scale = HD ** (-0.5)
    lane = lax.axis_index("tensor")
    first_item = lane * local_items
    live = (first_item + jnp.arange(local_items) < item_counts[0]).astype(jnp.float32)[
        :, None, None
    ]
    index = lax.axis_index("dp")
    tags = lax.all_gather(jnp.stack([timesteps, labels]), "dp", axis=1, tiled=True)
    time_feat = time_features(tags[0]).astype(jnp.bfloat16)
    pre_hidden = jnp.dot(
        time_feat, time_weight, preferred_element_type=jnp.float32
    ) + time_bias.astype(jnp.float32)
    time_hidden = jax.nn.silu(pre_hidden).astype(jnp.bfloat16)
    condition = (
        jnp.dot(time_hidden, embed_weight, preferred_element_type=jnp.float32)
        + embed_bias.astype(jnp.float32)
        + jnp.take(class_table, tags[1], axis=0).astype(jnp.float32)
    )
    cond_act = jax.nn.silu(condition).astype(jnp.bfloat16)
    cond_act_here = lax.dynamic_slice_in_dim(cond_act, index * items, items, 0)
    condition_here = lax.dynamic_slice_in_dim(condition, index * items, items, 0)
    modulation_part = (
        jnp.einsum(
            "bd,dke->bke", cond_act_here, modulate_weight, preferred_element_type=jnp.float32
        )
        + modulate_bias.astype(jnp.float32)
    ).astype(jnp.bfloat16)
    modulation_local = lax.all_to_all(
        modulation_part, "tensor", split_axis=0, concat_axis=2, tiled=True
    ).astype(jnp.float32)
    local_parts = [modulation_local[:, which][:, None, :] for which in range(6)]
    attend_shift, attend_scale, attend_gate, feed_shift, feed_scale, feed_gate = local_parts
    positions = jnp.arange(length)
    token_local = tokens.astype(jnp.float32)
    normed_local, inverse_local = layer_norm(token_local)
    mod_in = lax.all_gather(
        (normed_local * (1.0 + attend_scale) + attend_shift).astype(jnp.bfloat16),
        "tensor",
        axis=0,
        tiled=True,
    )
    projected = jnp.einsum(
        "bld,dke->blke", mod_in, project_weight, preferred_element_type=jnp.float32
    )
    split = projected.reshape(items, length, 3, heads_here, HD)
    query_gain_f = query_gain.astype(jnp.float32)
    key_gain_f = key_gain.astype(jnp.float32)
    queries = head_prepare(split[:, :, 0], query_gain_f, positions).astype(jnp.bfloat16)
    keys = head_prepare(split[:, :, 1], key_gain_f, positions).astype(jnp.bfloat16)
    values = split[:, :, 2].astype(jnp.bfloat16)
    scores = (
        jnp.einsum("bqhd,bkhd->bhqk", queries, keys, preferred_element_type=jnp.float32) * scale
    )
    top = jnp.max(scores, axis=-1, keepdims=True)
    logsum = top + jnp.log(jnp.sum(jnp.exp(scores - top), axis=-1, keepdims=True))
    probs = jnp.exp(scores - logsum).astype(jnp.bfloat16)
    mixed = jnp.einsum("bhqk,bkhd->bqhd", probs, values, preferred_element_type=jnp.float32)
    mixed = mixed.reshape(items, length, heads_here * HD).astype(jnp.bfloat16)
    piece = mixed
    attend_branch = lax.psum_scatter(
        jnp.einsum("blh,hd->bld", piece, output_weight, preferred_element_type=jnp.float32).astype(
            jnp.bfloat16
        ),
        "tensor",
        scatter_dimension=0,
        tiled=True,
    ).astype(jnp.float32) + output_bias.astype(jnp.float32)
    residual = token_local + attend_gate * attend_branch
    normed_two, inverse_two = layer_norm(residual)
    mod_two = (normed_two * (1.0 + feed_scale) + feed_shift).astype(jnp.bfloat16)
    mod_two_all = lax.all_gather(mod_two, "tensor", axis=0, tiled=True)
    gate_up = jnp.einsum(
        "bld,dkf->blkf", mod_two_all, expand_weight, preferred_element_type=jnp.float32
    )
    gate = gate_up[:, :, 0]
    upper = gate_up[:, :, 1]
    hidden = (jax.nn.silu(gate) * upper).astype(jnp.bfloat16)
    piece = hidden
    feed_branch = lax.psum_scatter(
        jnp.einsum("blf,fd->bld", piece, down_weight, preferred_element_type=jnp.float32).astype(
            jnp.bfloat16
        ),
        "tensor",
        scatter_dimension=0,
        tiled=True,
    ).astype(jnp.float32) + down_bias.astype(jnp.float32)
    result = (live * (residual + feed_gate * feed_branch)).astype(jnp.bfloat16)
    out_grad = cotangent.astype(jnp.float32) * live
    branch_grad = (out_grad * feed_gate).astype(jnp.bfloat16)
    down_bias_part = jnp.sum(branch_grad.astype(jnp.float32), axis=(0, 1))
    piece = lax.all_gather(branch_grad, "tensor", axis=0, tiled=True)
    weight_total = jnp.einsum("blf,bld->fd", hidden, piece, preferred_element_type=jnp.float32)
    rows_grad = jnp.einsum("bld,fd->blf", piece, down_weight, preferred_element_type=jnp.float32)
    hidden_total = rows_grad
    down_grad = weight_total
    gate_up_grad = jnp.stack(
        [hidden_total * upper * silu_slope(gate), hidden_total * jax.nn.silu(gate)], axis=2
    ).astype(jnp.bfloat16)
    expand_grad = jnp.einsum(
        "bld,blkf->dkf", mod_two_all, gate_up_grad, preferred_element_type=jnp.float32
    )
    piece = gate_up_grad
    mod_two_grad = lax.psum_scatter(
        jnp.einsum(
            "blkf,dkf->bld", piece, expand_weight, preferred_element_type=jnp.float32
        ).astype(jnp.bfloat16),
        "tensor",
        scatter_dimension=0,
        tiled=True,
    ).astype(jnp.float32)
    residual_grad = out_grad + layer_norm_back(
        normed_two, inverse_two, mod_two_grad * (1.0 + feed_scale)
    )
    attend_grad = (residual_grad * attend_gate).astype(jnp.bfloat16)
    output_bias_part = jnp.sum(attend_grad.astype(jnp.float32), axis=(0, 1))
    piece = lax.all_gather(attend_grad, "tensor", axis=0, tiled=True)
    weight_total = jnp.einsum("blh,bld->hd", mixed, piece, preferred_element_type=jnp.float32)
    rows_grad = jnp.einsum("bld,hd->blh", piece, output_weight, preferred_element_type=jnp.float32)
    output_weight_grad = weight_total
    mixed_grad = rows_grad
    mixed_grad = mixed_grad.reshape(items, length, heads_here, HD).astype(jnp.bfloat16)
    again = jnp.einsum("bqhd,bkhd->bhqk", queries, keys, preferred_element_type=jnp.float32) * scale
    prob_float = jnp.exp(again - logsum)
    prob_low = prob_float.astype(jnp.bfloat16)
    prob_grad = jnp.einsum(
        "bqhd,bkhd->bhqk", mixed_grad, values, preferred_element_type=jnp.float32
    )
    score_grad = (
        prob_float * (prob_grad - jnp.sum(prob_float * prob_grad, axis=-1, keepdims=True))
    ).astype(jnp.bfloat16)
    query_grad = (
        jnp.einsum("bhqk,bkhd->bqhd", score_grad, keys, preferred_element_type=jnp.float32) * scale
    )
    key_grad = (
        jnp.einsum("bhqk,bqhd->bkhd", score_grad, queries, preferred_element_type=jnp.float32)
        * scale
    )
    value_grad = jnp.einsum(
        "bhqk,bqhd->bkhd", prob_low, mixed_grad, preferred_element_type=jnp.float32
    )

    def prepare_here(raw, gain):
        return head_prepare(raw, gain, positions)

    _, query_back = jax.vjp(prepare_here, split[:, :, 0], query_gain_f)
    raw_query_grad, query_gain_part = query_back(query_grad)
    _, key_back = jax.vjp(prepare_here, split[:, :, 1], key_gain_f)
    raw_key_grad, key_gain_part = key_back(key_grad)
    projected_grad = jnp.stack([raw_query_grad, raw_key_grad, value_grad], axis=2)
    projected_grad = projected_grad.reshape(items, length, 3, heads_here * HD).astype(jnp.bfloat16)
    project_grad = jnp.einsum(
        "bld,blke->dke", mod_in, projected_grad, preferred_element_type=jnp.float32
    )
    piece = projected_grad
    mod_in_grad = lax.psum_scatter(
        jnp.einsum(
            "blke,dke->bld", piece, project_weight, preferred_element_type=jnp.float32
        ).astype(jnp.bfloat16),
        "tensor",
        scatter_dimension=0,
        tiled=True,
    ).astype(jnp.float32)
    tokens_grad = (
        residual_grad
        + layer_norm_back(normed_local, inverse_local, mod_in_grad * (1.0 + attend_scale))
    ).astype(jnp.bfloat16)
    modulation_grad_part = jnp.stack(
        [
            jnp.sum(mod_in_grad, axis=1),
            jnp.sum(mod_in_grad * normed_local, axis=1),
            jnp.sum(residual_grad * attend_branch, axis=1),
            jnp.sum(mod_two_grad, axis=1),
            jnp.sum(mod_two_grad * normed_two, axis=1),
            jnp.sum(out_grad * feed_branch, axis=1),
        ],
        axis=1,
    )
    modulation_grad = lax.all_to_all(
        modulation_grad_part, "tensor", split_axis=2, concat_axis=0, tiled=True
    ).astype(jnp.bfloat16)
    modulate_bias_part = jnp.sum(modulation_grad.astype(jnp.float32), axis=0)
    cond_part = jnp.einsum(
        "bke,dke->bd", modulation_grad, modulate_weight, preferred_element_type=jnp.float32
    )
    cond_total = lax.psum(cond_part, "tensor")
    cond_grad_here = (cond_total * silu_slope(condition_here)).astype(jnp.bfloat16)
    packed = jnp.concatenate([cond_grad_here, modulation_grad.reshape(items, 6 * slab)], axis=1)
    packed = lax.all_gather(packed, "dp", axis=0, tiled=True)
    cond_grad = packed[:, :width]
    modulation_grad_all = packed[:, width:].reshape(-1, 6, slab)
    share = width // lax.axis_size("dp")

    def mine(value, axis):
        return lax.dynamic_slice_in_dim(value, index * share, share, axis)

    one_hot = (tags[1][:, None] == jnp.arange(class_table.shape[0])[None, :]).astype(jnp.bfloat16)
    cond_grad_mine = mine(cond_grad, 1)
    class_grad = jnp.einsum(
        "bc,bd->cd", one_hot, cond_grad_mine, preferred_element_type=jnp.float32
    )
    pre_grad = (
        jnp.einsum(
            "be,de->bd", cond_grad, mine(embed_weight, 0), preferred_element_type=jnp.float32
        )
        * silu_slope(mine(pre_hidden, 1))
    ).astype(jnp.bfloat16)
    modulate_grad = jnp.einsum(
        "bd,bke->dke", mine(cond_act, 1), modulation_grad_all, preferred_element_type=jnp.float32
    )
    embed_grad = jnp.einsum(
        "bd,be->de", mine(time_hidden, 1), cond_grad, preferred_element_type=jnp.float32
    )
    embed_bias_grad = jnp.sum(cond_grad_mine.astype(jnp.float32), axis=0)
    time_grad = jnp.einsum("bf,bd->fd", time_feat, pre_grad, preferred_element_type=jnp.float32)
    time_bias_grad = jnp.sum(pre_grad.astype(jnp.float32), axis=0)
    bias_wide = lax.dynamic_update_slice_in_dim(
        jnp.zeros((6, width), jnp.float32), modulate_bias_part, lane * slab, 1
    )
    small = jnp.concatenate(
        [output_bias_part, down_bias_part, bias_wide.reshape(-1), query_gain_part, key_gain_part]
    )
    small = lax.psum(small, ("dp", "tensor"))
    output_bias_grad = small[:width]
    down_bias_grad = small[width : 2 * width]
    modulate_bias_grad = small[2 * width : 8 * width].reshape(6, width)
    query_gain_grad = small[8 * width : 8 * width + HD]
    key_gain_grad = small[8 * width + HD :]

    def scatter(value, axis):
        value = value.astype(jnp.bfloat16)
        return lax.psum_scatter(value, "dp", scatter_dimension=axis, tiled=True).astype(jnp.float32)

    project_grad = scatter(project_grad, 0)
    output_weight_grad = scatter(output_weight_grad, 1)
    expand_grad = scatter(expand_grad, 0)
    down_grad = scatter(down_grad, 1)
    return (
        result,
        tokens_grad,
        project_grad,
        query_gain_grad,
        key_gain_grad,
        output_weight_grad,
        output_bias_grad,
        expand_grad,
        down_grad,
        down_bias_grad,
        modulate_grad,
        modulate_bias_grad,
        time_grad,
        time_bias_grad,
        embed_grad,
        embed_bias_grad,
        class_grad,
    )


def solution(mesh):
    return jax.shard_map(
        shards,
        mesh=mesh,
        in_specs=(
            P(("dp", "tensor"), None, None),
            P("dp"),
            P("dp"),
            P("dp"),
            P(("dp", "tensor"), None, None),
            P(None, None, "tensor"),
            P(),
            P(),
            P("tensor", None),
            P(),
            P(None, None, "tensor"),
            P("tensor", None),
            P(),
            P(None, None, "tensor"),
            P(None, "tensor"),
            P(),
            P(),
            P(),
            P(),
            P(),
        ),
        out_specs=(
            P(("dp", "tensor"), None, None),
            P(("dp", "tensor"), None, None),
            P("dp", None, "tensor"),
            P(),
            P(),
            P("tensor", "dp"),
            P(),
            P("dp", None, "tensor"),
            P("tensor", "dp"),
            P(),
            P("dp", None, "tensor"),
            P(),
            P(None, "dp"),
            P("dp"),
            P("dp", None),
            P("dp"),
            P(None, "dp"),
        ),
        check_vma=False,
    )
```

profile of v0, /device:TPU:0, one launch (start us, length us, event | category | flops | bytes accessed | tf_op | source)
XLA Modules:
  0.0 764.2 jit_solution(1192706459011180409)
XLA Ops:
  8.1 10.4 %all-gather = s32[8,4,2]{1,2,0:T(2,128)S(1)} all-gather(s32[1,4,2]{1,2,0:T(2,128)S(1)} %add_bitcast_fusion), channel_id=1, replica_groups=mesh['dp'=8,'tensor'=4] {'dp'}, dimensions={0}, use_global_device_ids=true | all-gather | bytes 288 | tf_op jit(solution)/shard_map/all_gather | solution.py:94
  21.4 2.6 gather_fusion
  24.0 2.1 multiply_convert_fusion.8
  26.2 1.2 multiply_convert_fusion.7
  27.4 1.3 fusion.49
  29.4 4.9 all-to-all-start
  34.8 5.1 all-to-all-done
  42.8 47.1 %all-gather.7.cloned.1.call-done = bf16[4,256,1152]{2,1,0:T(8,128)(2,1)} async-done(((bf16[1,256,1152]{2,1,0:T(8,128)(2,1)}), bf16[4,256,1152]{2,1,0:T(8,128)(2,1)}) %all-gather.7.cloned.1.call-update) | async-done | bytes 2359312 | tf_op jit(solution)/shard_map/all_gather | solution.py:122
  90.0 4.7 fusion.10
  98.6 1.2 multiply_reduce_fusion.1
  100.6 1.3 copy-done.1
  103.5 2.9 convolution_convert_fusion.1
  106.6 1.3 convert_element_type.316
  107.8 45.3 %reduce-scatter.9.cloned.1.call-done = bf16[1,256,1152]{2,1,0:T(8,128)(2,1)} async-done(((bf16[4,256,1152]{2,1,0:T(8,128)(2,1)}), bf16[1,256,1152]{2,1,0:T(8,128)(2,1)}) %reduce-scatter.9.cloned.1.call-update) | async-done | bytes 589840 | tf_op jit(solution)/shard_map/reduce_scatter | solution.py:146
  153.1 1.4 fusion.103
  155.6 1.2 add_convert_fusion
  157.6 2.7 convert_reduce_fusion.3
  160.6 45.8 %all-gather.9.cloned.1.call-done = bf16[4,256,1152]{2,1,0:T(8,128)(2,1)} async-done(((bf16[1,256,1152]{2,1,0:T(8,128)(2,1)}), bf16[4,256,1152]{2,1,0:T(8,128)(2,1)}) %all-gather.9.cloned.1.call-update) | async-done | bytes 2359312 | tf_op jit(solution)/shard_map/all_gather | solution.py:157
  206.4 9.6 %fusion.1 = f32[4,256,2,768]{3,1,2,0:T(8,128)} fusion(bf16[1152,2,768]{2,1,0:T(2,128)(2,1)} %param.30, bf16[4,256,1152]{2,1,0:T(8,128)(2,1)} %all-gather.9.cloned.1.call-done), kind=kOutput, calls=%fused_computation.14 | convolution fusion | flops 3623878656 | bytes 12189696 | tf_op jit(solution)/shard_map/bld,dkf->blkf/dot_general | solution.py:158
  216.0 41.2 %all-gather.11.cloned.1.call-done = bf16[4,256,1152]{2,1,0:T(8,128)(2,1)} async-done(((bf16[1,256,1152]{2,1,0:T(8,128)(2,1)}), bf16[4,256,1152]{2,1,0:T(8,128)(2,1)}) %all-gather.11.cloned.1.call-update) | async-done | bytes 2359312 | tf_op jit(solution)/shard_map/all_gather | solution.py:177
  257.2 8.4 %fusion.26 = (bf16[4,256,1,768]{3,1,0,2:T(8,128)(2,1)S(1)}, bf16[4,256,1,768]{3,1,0,2:T(8,128)(2,1)S(1)}, bf16[4,256,768]{2,1,0:T(8,128)(2,1)}) fusion(f32[4,256,2,768]{3,1,2,0:T(8,128)} %fusion.1, bf16[4,256,1152]{2,1,0:T(8,128)(2,1)} %all-gather.11.cloned.1.call-done, bf16[768,1152]{1,0:T(8,128)(2,1)} %param.31), kind=kOutput, calls=%fused_computation.62 | convolution fusion | flops 1823735808 | bytes 15138816 | tf_op jit(solution)/shard_map/bld,fd->blf/dot_general | solution.py:179
  265.6 1.2 copy-done.81
  267.2 5.6 bitcast_convert_fusion.3
  272.8 5.6 convolution_convert_fusion
  278.5 1.3 convert_element_type.321
  279.8 39.6 %reduce-scatter.13.cloned.1.call-done = bf16[1,256,1152]{2,1,0:T(8,128)(2,1)} async-done(((bf16[4,256,1152]{2,1,0:T(8,128)(2,1)}), bf16[1,256,1152]{2,1,0:T(8,128)(2,1)}) %reduce-scatter.13.cloned.1.call-update) | async-done | bytes 589840 | tf_op jit(solution)/shard_map/reduce_scatter | solution.py:189
  319.4 2.6 fusion.45
  323.2 45.5 %reduce-scatter.11.cloned.1.call-done = bf16[1,256,1152]{2,1,0:T(8,128)(2,1)} async-done(((bf16[4,256,1152]{2,1,0:T(8,128)(2,1)}), bf16[1,256,1152]{2,1,0:T(8,128)(2,1)}) %reduce-scatter.11.cloned.1.call-update) | async-done | bytes 589840 | tf_op jit(solution)/shard_map/reduce_scatter | solution.py:165
  368.7 4.1 multiply_reduce_fusion.5
  373.9 1.5 convert_reduce_fusion.4
  375.4 11.2 %reduce-scatter.23.cloned.1.call-start = ((), (), s32[]{:S(2)}) async-start(), calls=%async_computation.21 | async-start | bytes 1990656 | tf_op jit(solution)/shard_map/reduce_scatter | solution.py:317
  386.6 5.4 fusion.4
  392.1 8.2 %bitcast_convert_fusion = bf16[1152,2,768]{2,0,1:T(8,128)(2,1)} fusion(bf16[4,256,1152]{2,1,0:T(8,128)(2,1)} %all-gather.9.cloned.1.call-done, bf16[4,256,1,768]{3,1,0,2:T(8,128)(2,1)} %copy-done.82, bf16[4,256,1,768]{3,1,0,2:T(8,128)(2,1)} %copy-done.81), kind=kOutput, calls=%fused_computation.1 | convolution fusion | flops 3631939584 | bytes 9043968 | tf_op jit(solution)/shard_map/bld,blkf->dkf/dot_general | solution.py:185
  400.4 24.6 %all-gather.13.cloned.1.call-done = bf16[4,256,1152]{2,1,0:T(8,128)(2,1)} async-done(((bf16[1,256,1152]{2,1,0:T(8,128)(2,1)}), bf16[4,256,1152]{2,1,0:T(8,128)(2,1)}) %all-gather.13.cloned.1.call-update) | async-done | bytes 2359312 | tf_op jit(solution)/shard_map/all_gather | solution.py:202
  424.9 2.9 convolution_convert_fusion.3
  428.0 2.4 multiply_reduce_fusion
  438.8 1.2 fusion.47
  440.9 2.4 fusion.6
  443.3 2.0 fusion.46
  445.4 3.5 convolution_convert_fusion.2
  449.8 5.3 bitcast_convert_fusion.1
  455.4 6.5 bitcast_convert_fusion.2
  461.9 4.4 reduce-scatter.23.cloned.1.call-done
  466.3 1.7 convert_element_type.348
  468.1 49.6 %reduce-scatter.21.cloned.1.call-done = bf16[144,2,768]{2,0,1:T(8,128)(2,1)} async-done(((bf16[1152,2,768]{2,0,1:T(8,128)(2,1)}), bf16[144,2,768]{2,0,1:T(8,128)(2,1)}) %reduce-scatter.21.cloned.1.call-update) | async-done | bytes 442384 | tf_op jit(solution)/shard_map/reduce_scatter | solution.py:317
  517.7 2.3 copy.157
  520.0 35.5 %reduce-scatter.19.cloned.1.call-done = bf16[288,144]{0,1:T(8,128)(2,1)} async-done(((bf16[288,1152]{0,1:T(8,128)(2,1)}), bf16[288,144]{0,1:T(8,128)(2,1)}) %reduce-scatter.19.cloned.1.call-update) | async-done | bytes 82960 | tf_op jit(solution)/shard_map/reduce_scatter | solution.py:317
  555.4 1.6 convert_element_type.344
  557.0 44.9 %reduce-scatter.17.cloned.1.call-done = bf16[144,3,288]{2,0,1:T(8,128)(2,1)} async-done(((bf16[1152,3,288]{2,0,1:T(8,128)(2,1)}), bf16[144,3,288]{2,0,1:T(8,128)(2,1)}) %reduce-scatter.17.cloned.1.call-update) | async-done | bytes 248848 | tf_op jit(solution)/shard_map/reduce_scatter | solution.py:317
  602.0 1.9 convert_element_type.335
  603.8 48.0 %reduce-scatter.15.cloned.1.call-done = bf16[1,256,1152]{2,1,0:T(8,128)(2,1)} async-done(((bf16[4,256,1152]{2,1,0:T(8,128)(2,1)}), bf16[1,256,1152]{2,1,0:T(8,128)(2,1)}) %reduce-scatter.15.cloned.1.call-update) | async-done | bytes 589840 | tf_op jit(solution)/shard_map/reduce_scatter | solution.py:241
  651.9 1.7 fusion.48
  654.7 1.3 copy.150
  656.5 7.7 %reduce.26 = bf16[1152,6]{1,0:T(8,128)(2,1)S(1)} reduce(bf16[1152,1,6]{2,1,0:T(2,128)(2,1)} %bitcast.210, bf16[]{:T(256)} %broadcast.432), dimensions={1}, to_apply=%bitcast.178.reduce_sub_computation | reduce | bytes 27650
  665.2 3.3 all-to-all-start.1
  668.5 2.8 fusion.38
  671.2 2.8 all-to-all-done.1
  675.8 39.6 %psum.14 = f32[9360]{0:T(1024)S(1)} all-reduce(f32[9360]{0:T(1024)S(1)} %concatenate.23), channel_id=1, replica_groups=mesh['dp'=8,'tensor'=4] {'dp','tensor'}, use_global_device_ids=true, to_apply=%region_31.32 | all-reduce | flops 9360 | bytes 74880 | tf_op jit(solution)/shard_map/psum | solution.py:308
  716.6 2.8 convolution_bitcast_fusion.2
  719.4 17.1 %psum.15 = f32[4,1152]{1,0:T(4,128)S(1)} all-reduce(f32[4,1152]{1,0:T(4,128)S(1)} %convolution_bitcast_fusion.2), channel_id=1, replica_groups=mesh['dp'=8,'tensor'=4] {'tensor'}, use_global_device_ids=true, to_apply=%region_35.36 | all-reduce | flops 4608 | bytes 36864 | tf_op jit(solution)/shard_map/psum | solution.py:271
  737.5 10.0 %all-gather.1 = bf16[8,4,2880]{2,1,0:T(4,128)(2,1)S(1)} all-gather(bf16[1,4,2880]{2,1,0:T(4,128)(2,1)S(1)} %maximum_bitcast_fusion), channel_id=1, replica_groups=mesh['dp'=8,'tensor'=4] {'dp'}, dimensions={0}, use_global_device_ids=true | all-gather | bytes 207360 | tf_op jit(solution)/shard_map/all_gather | solution.py:274
  748.3 1.9 fusion.68
  750.2 1.6 convert_reduce_fusion.7
  754.7 2.2 fusion.60
  (277 shorter events, 38.6 us)
Async XLA Ops:
  7.2 19.0 %copy-start = (bf16[1152,1152]{1,0:T(8,128)(2,1)S(1)}, bf16[1152,1152]{1,0:T(8,128)(2,1)}, u32[]{:S(2)}) copy-start(bf16[1152,1152]{1,0:T(8,128)(2,1)} %param.37) | copy-start | bytes 7962628
  21.4 6.0 copy-start.54
  21.4 6.0 copy-start.56
  24.0 3.4 copy-start.8
  27.4 6.9 copy-start.3
  29.4 10.5 %all-to-all-start = ((bf16[4,6,288]{2,1,0:T(8,128)(2,1)}), bf16[4,6,288]{2,1,0:T(8,128)(2,1)S(1)}, u32[]{:S(2)}, u32[]{:S(2)}) async-start(bf16[4,6,288]{2,1,0:T(8,128)(2,1)} %copy.133), calls=%async_computation | async-start | bytes 49152 | tf_op jit(solution)/shard_map/all_to_all | solution.py:114
  34.3 55.7 %all-gather.7.cloned.1.call-start = ((), (), s32[]{:S(2)}) async-start(), calls=%async_computation.10 | async-start | bytes 2949120 | tf_op jit(solution)/shard_map/all_gather | solution.py:122
  34.4 8.0 %copy-start.58 = (f32[256]{0:T(256)}, f32[256]{0:T(256)S(1)}, u32[]{:S(2)}) copy-start(f32[256]{0:T(256)S(1)} %broadcast_multiply_fusion.5) | copy-start | bytes 3076
  34.8 7.7 %copy-start.79 = (bf16[72]{0:T(256)(128)(2,1)S(1)}, bf16[72]{0:T(256)(128)(2,1)}, u32[]{:S(2)}) copy-start(bf16[72]{0:T(256)(128)(2,1)} %param.26) | copy-start | bytes 436
  34.8 7.7 %copy-start.80 = (bf16[72]{0:T(256)(128)(2,1)S(1)}, bf16[72]{0:T(256)(128)(2,1)}, u32[]{:S(2)}) copy-start(bf16[72]{0:T(256)(128)(2,1)} %param.27) | copy-start | bytes 436
  34.8 59.9 %copy-start.61 = (f32[256]{0:T(256)}, f32[256]{0:T(256)S(1)}, u32[]{:S(2)}) copy-start(f32[256]{0:T(256)S(1)} %add_rsqrt_fusion.1) | copy-start | bytes 3076
  42.4 110.7 %reduce-scatter.9.cloned.1.call-start = ((), (), s32[]{:S(2)}) async-start(), calls=%async_computation.11 | async-start | bytes 2949120 | tf_op jit(solution)/shard_map/reduce_scatter | solution.py:146
  42.5 52.8 %copy-start.68 = (f32[72]{0:T(128)}, f32[72]{0:T(128)S(1)}, u32[]{:S(2)}) copy-start(f32[72]{0:T(128)S(1)} %convert_element_type.306) | copy-start | bytes 868
  42.5 53.9 %copy-start.70 = (f32[72]{0:T(128)}, f32[72]{0:T(128)S(1)}, u32[]{:S(2)}) copy-start(f32[72]{0:T(128)S(1)} %convert_element_type.309) | copy-start | bytes 868
  94.7 5.9 copy-start.11
  95.0 1.7 copy-start.6
  98.1 1.6 copy-start.22
  98.1 1.6 copy-start.24
  98.2 1.6 copy-start.26
  98.2 1.6 copy-start.28
  99.8 2.0 copy-start.1
  101.9 1.7 copy-start.78
  106.5 99.9 %all-gather.9.cloned.1.call-start = ((), (), s32[]{:S(2)}) async-start(), calls=%async_computation.12 | async-start | bytes 2949120 | tf_op jit(solution)/shard_map/all_gather | solution.py:157
  153.1 1.5 copy-start.37
  153.1 2.5 copy-start.49
  153.1 2.5 copy-start.51
  156.9 100.3 %all-gather.11.cloned.1.call-start = ((), (), s32[]{:S(2)}) async-start(), calls=%async_computation.14 | async-start | bytes 2949120 | tf_op jit(solution)/shard_map/all_gather | solution.py:177
  160.3 159.2 %reduce-scatter.13.cloned.1.call-start = ((), (), s32[]{:S(2)}) async-start(), calls=%async_computation.15 | async-start | bytes 2949120 | tf_op jit(solution)/shard_map/reduce_scatter | solution.py:189
  257.2 10.0 %copy-start.75 = (bf16[1152,2,768]{2,1,0:T(2,128)(2,1)S(1)}, bf16[1152,2,768]{2,1,0:T(2,128)(2,1)}, u32[]{:S(2)}) copy-start(bf16[1152,2,768]{2,1,0:T(2,128)(2,1)} %param.30) | copy-start | bytes 10616836
  265.6 1.6 copy-start.82
  272.8 95.9 %reduce-scatter.11.cloned.1.call-start = ((), (), s32[]{:S(2)}) async-start(), calls=%async_computation.13 | async-start | bytes 2949120 | tf_op jit(solution)/shard_map/reduce_scatter | solution.py:165
  278.5 146.5 %all-gather.13.cloned.1.call-start = ((), (), s32[]{:S(2)}) async-start(), calls=%async_computation.16 | async-start | bytes 2949120 | tf_op jit(solution)/shard_map/all_gather | solution.py:202
  368.7 5.2 copy-start.36
  375.4 90.9 %reduce-scatter.23.cloned.1.call-start = ((), (), s32[]{:S(2)}) async-start(), calls=%async_computation.21 | async-start | bytes 1990656 | tf_op jit(solution)/shard_map/reduce_scatter | solution.py:317
  392.0 125.7 %reduce-scatter.21.cloned.1.call-start = ((), (), s32[]{:S(2)}) async-start(), calls=%async_computation.20 | async-start | bytes 3981312 | tf_op jit(solution)/shard_map/reduce_scatter | solution.py:317
  400.3 155.1 %reduce-scatter.19.cloned.1.call-start = ((), (), s32[]{:S(2)}) async-start(), calls=%async_computation.19 | async-start | bytes 995328 | tf_op jit(solution)/shard_map/reduce_scatter | solution.py:317
  424.9 3.1 copy-start.2
  427.8 2.6 copy-start.14
  433.6 3.5 copy-start.12
  436.0 1.6 copy-start.5
  436.0 1.6 copy-start.39
  436.1 1.6 copy-start.69
  438.8 2.1 copy-start.77
  443.3 158.7 %reduce-scatter.17.cloned.1.call-start = ((), (), s32[]{:S(2)}) async-start(), calls=%async_computation.18 | async-start | bytes 2985984 | tf_op jit(solution)/shard_map/reduce_scatter | solution.py:317
  443.3 2.0 copy-start.15
  445.4 3.6 copy-start.33
  445.4 4.4 copy-start.32
  445.4 4.3 copy-start.76
  455.1 196.7 %reduce-scatter.15.cloned.1.call-start = ((), (), s32[]{:S(2)}) async-start(), calls=%async_computation.17 | async-start | bytes 2949120 | tf_op jit(solution)/shard_map/reduce_scatter | solution.py:241
  461.9 6.2 copy-start.64
  461.9 6.2 copy-start.63
  461.9 6.2 copy-start.67
  461.9 6.2 copy-start.66
  468.1 183.7 %copy-start.48 = (f32[1152]{0:T(1024)S(1)}, f32[1152]{0:T(1024)}, u32[]{:S(2)}) copy-start(f32[1152]{0:T(1024)} %copy-done.47) | copy-start | bytes 13828
  468.1 183.7 %copy-start.59 = (f32[256]{0:T(256)S(1)}, f32[256]{0:T(256)}, u32[]{:S(2)}) copy-start(f32[256]{0:T(256)} %copy-done.58) | copy-start | bytes 3076
  468.1 183.7 %copy-start.62 = (f32[256]{0:T(256)S(1)}, f32[256]{0:T(256)}, u32[]{:S(2)}) copy-start(f32[256]{0:T(256)} %copy-done.61) | copy-start | bytes 3076
  665.2 8.8 %all-to-all-start.1 = ((bf16[4,2,864]{2,1,0:T(2,128)(2,1)}), bf16[4,2,864]{2,1,0:T(2,128)(2,1)S(1)}, u32[]{:S(2)}, u32[]{:S(2)}) async-start(bf16[4,2,864]{2,1,0:T(2,128)(2,1)} %reshape.475), calls=%async_computation.6 | async-start | bytes 28672 | tf_op jit(solution)/shard_map/all_to_all | solution.py:264
  671.2 4.5 copy-start.52
  671.2 4.5 copy-start.53
  671.2 4.5 copy-start.72
  671.2 4.5 copy-start.73
  747.5 5.2 copy-start.55
  747.5 5.2 copy-start.57
  747.6 6.0 copy-start.74
  (33 other events, 36.0 us)
Sparse Core Ops, SparseCore 0:
  42.5 47.3 all-gather.6
  106.6 46.4 reduce-scatter.8
  157.0 49.3 all-gather.8
  208.4 48.7 all-gather.10
  272.9 46.4 reduce-scatter.12
  321.6 47.0 reduce-scatter.10
  375.5 49.3 all-gather.12
  428.3 37.9 reduce-scatter.22
  469.8 47.8 reduce-scatter.20
  520.8 34.6 reduce-scatter.18
  558.9 42.9 reduce-scatter.16
  604.1 47.6 reduce-scatter.14
where the time goes:
time: 774 us; the launch traced here: 764 us
  waiting for transfers between devices  480 us (62%)
  matrix products  92 us (12%)
  blocking collectives  77.2 us (10%)
  other arithmetic  53.3 us (7%)
  local copies, waits for them, and re-layouts  25.5 us (3%)
  starting transfers between devices  20.2 us (3%)
  between operations  16.4 us (2%)
    reduce_scatter x4, waiting for transfers between devices, scatter(): lax.psum_scatter(value, 'dp', scatter_dimension=axis, tiled=True)  134 us
    reduce_scatter x1, waiting for transfers between devices, shards(): lax.psum_scatter(jnp.einsum('blke,dke->bld', piece, project_weight, prefe...  48 us
    all_gather x1, waiting for transfers between devices, shards(): lax.all_gather((normed_local * (1.0 + attend_scale) + attend_shift).astyp...  47.1 us
    all_gather x1, waiting for transfers between devices, shards(): mod_two_all = lax.all_gather(mod_two, 'tensor', axis=0, tiled=True)  45.8 us
    reduce_scatter x1, waiting for transfers between devices, shards(): lax.psum_scatter(jnp.einsum('blf,fd->bld', piece, down_weight, preferred_...  45.5 us
    reduce_scatter x1, waiting for transfers between devices, shards(): lax.psum_scatter(jnp.einsum('blh,hd->bld', piece, output_weight, preferre...  45.3 us
    all_gather x1, waiting for transfers between devices, shards(): piece = lax.all_gather(branch_grad, 'tensor', axis=0, tiled=True)  41.2 us
    psum x1, blocking collectives, shards(): small = lax.psum(small, ('dp', 'tensor'))  39.6 us
  transfers between devices with their start and end apart: 14, of which 14 were waited for; matrix products, arithmetic and copies ran while one was open for 11% of the time, Pallas kernels for 0%

commit v1 on v0

--- a/solution.py
+++ b/solution.py
@@ -199,7 +199,33 @@
     )
     attend_grad = (residual_grad * attend_gate).astype(jnp.bfloat16)
     output_bias_part = jnp.sum(attend_grad.astype(jnp.float32), axis=(0, 1))
-    piece = lax.all_gather(attend_grad, "tensor", axis=0, tiled=True)
+    arr_next, raw_out, response = (
+        lax.axis_size("tensor"),
+        lax.axis_index("tensor"),
+        attend_grad.shape[0],
+    )
+    by_rank = [nth * arr_next if src_i == 0 else nth for src_i, nth in enumerate(attend_grad.shape)]
+    low = jnp.zeros(by_rank, attend_grad.dtype)
+    piece = lax.dynamic_update_slice_in_dim(low, attend_grad, raw_out * response, axis=0)
+    val2 = part_now = attend_grad
+    for j in range(1, arr_next // 2 + 1):
+        val2 = lax.ppermute(
+            val2,
+            axis_name="tensor",
+            perm=[(src_i, (src_i + 1) % arr_next) for src_i in range(arr_next)],
+        )
+        piece = lax.dynamic_update_slice_in_dim(
+            piece, val2, (raw_out - j) % arr_next * response, axis=0
+        )
+        if 2 * j < arr_next:
+            part_now = lax.ppermute(
+                part_now,
+                axis_name="tensor",
+                perm=[(src_i, (src_i - 1) % arr_next) for src_i in range(arr_next)],
+            )
+            piece = lax.dynamic_update_slice_in_dim(
+                piece, part_now, (raw_out + j) % arr_next * response, axis=0
+            )
     weight_total = jnp.einsum("blh,bld->hd", mixed, piece, preferred_element_type=jnp.float32)
     rows_grad = jnp.einsum("bld,hd->blh", piece, output_weight, preferred_element_type=jnp.float32)
     output_weight_grad = weight_total

time: 774 us -> 716 us (0.925)
  waiting for transfers between devices: 480 us -> 415 us
  local copies, waits for them, and re-layouts: 25.5 us -> 40.9 us
    reduce_scatter x4, waiting for transfers between devices: 134 us -> 80.6 us  [scatter(): lax.psum_scatter(value, 'dp', scatter_dimension=axis, tiled=True)]
    all_gather x1 -> x0, waiting for transfers between devices: 24.6 us -> none  [shards(): piece = lax.all_gather(attend_grad, 'tensor', axis=0, tiled=True)]
    ppermute x0 -> x3, waiting for transfers between devices: none -> 20.6 us  [the longest x2 15 us: shards(): lax.ppermute(val2, axis_name='tensor', perm=[(src_i, (src_i + 1) % arr_ne...]
    reduce_scatter x4, starting transfers between devices: 11.3 us -> 0.17 us  [scatter(): lax.psum_scatter(value, 'dp', scatter_dimension=axis, tiled=True)]
    unnamed x172 -> x182, local copies, waits for them, and re-layouts: 17.4 us -> 16.9 us
  transfers between devices with their start and end apart: 14 -> 16, of which waited for: 14 -> 15; matrix products, arithmetic and copies ran while one was open for 11% -> 15% of each run, Pallas kernels for 0% -> 0%
where the time goes in v1:
time: 716 us; the launch traced here: 706 us
  waiting for transfers between devices  415 us (58%)
  matrix products  91.2 us (13%)
  blocking collectives  75.5 us (11%)
  other arithmetic  54.3 us (8%)
  local copies, waits for them, and re-layouts  40.9 us (6%)
  between operations  16 us (2%)
  starting transfers between devices  13.1 us (2%)
    reduce_scatter x4, waiting for transfers between devices, scatter(): lax.psum_scatter(value, 'dp', scatter_dimension=axis, tiled=True)  80.6 us
    reduce_scatter x1, waiting for transfers between devices, shards(): lax.psum_scatter(jnp.einsum('blke,dke->bld', piece, project_weight, prefe...  48.2 us
    all_gather x1, waiting for transfers between devices, shards(): lax.all_gather((normed_local * (1.0 + attend_scale) + attend_shift).astyp...  47.1 us
    all_gather x1, waiting for transfers between devices, shards(): mod_two_all = lax.all_gather(mod_two, 'tensor', axis=0, tiled=True)  45.9 us
    reduce_scatter x1, waiting for transfers between devices, shards(): lax.psum_scatter(jnp.einsum('blf,fd->bld', piece, down_weight, preferred_...  45.5 us
    reduce_scatter x1, waiting for transfers between devices, shards(): lax.psum_scatter(jnp.einsum('blh,hd->bld', piece, output_weight, preferre...  45.3 us
    all_gather x1, waiting for transfers between devices, shards(): piece = lax.all_gather(branch_grad, 'tensor', axis=0, tiled=True)  41.2 us
    psum x1, blocking collectives, shards(): small = lax.psum(small, ('dp', 'tensor'))  37.9 us
  transfers between devices with their start and end apart: 16, of which 15 were waited for; matrix products, arithmetic and copies ran while one was open for 15% of the time, Pallas kernels for 0%

profile of v1, /device:TPU:0, one launch (start us, length us, event | category | flops | bytes accessed | tf_op | source)
XLA Modules:
  0.0 706.2 jit_solution(5829355002493686431)
XLA Ops:
  8.1 10.4 %all-gather = s32[8,4,2]{1,2,0:T(2,128)S(1)} all-gather(s32[1,4,2]{1,2,0:T(2,128)S(1)} %add_bitcast_fusion), channel_id=1, replica_groups=mesh['dp'=8,'tensor'=4] {'dp'}, dimensions={0}, use_global_device_ids=true | all-gather | bytes 288 | tf_op jit(solution)/shard_map/all_gather | solution.py:94
  21.4 2.6 gather_fusion
  24.1 2.1 multiply_convert_fusion.8
  27.4 1.3 fusion.49
  29.4 4.9 all-to-all-start
  34.8 5.1 all-to-all-done
  42.9 47.1 %all-gather.6.cloned.1.call-done = bf16[4,256,1152]{2,1,0:T(8,128)(2,1)} async-done(((bf16[1,256,1152]{2,1,0:T(8,128)(2,1)}), bf16[4,256,1152]{2,1,0:T(8,128)(2,1)}) %all-gather.6.cloned.1.call-update) | async-done | bytes 2359312 | tf_op jit(solution)/shard_map/all_gather | solution.py:122
  90.0 4.7 fusion.10
  103.6 2.9 convolution_convert_fusion.1
  107.9 45.3 %reduce-scatter.9.cloned.1.call-done = bf16[1,256,1152]{2,1,0:T(8,128)(2,1)} async-done(((bf16[4,256,1152]{2,1,0:T(8,128)(2,1)}), bf16[1,256,1152]{2,1,0:T(8,128)(2,1)}) %reduce-scatter.9.cloned.1.call-update) | async-done | bytes 589840 | tf_op jit(solution)/shard_map/reduce_scatter | solution.py:146
  153.2 1.4 fusion.103
  157.6 2.7 convert_reduce_fusion.3
  160.5 45.9 %all-gather.8.cloned.1.call-done = bf16[4,256,1152]{2,1,0:T(8,128)(2,1)} async-done(((bf16[1,256,1152]{2,1,0:T(8,128)(2,1)}), bf16[4,256,1152]{2,1,0:T(8,128)(2,1)}) %all-gather.8.cloned.1.call-update) | async-done | bytes 2359312 | tf_op jit(solution)/shard_map/all_gather | solution.py:157
  206.4 9.6 %fusion.1 = f32[4,256,2,768]{3,1,2,0:T(8,128)} fusion(bf16[1152,2,768]{2,1,0:T(2,128)(2,1)} %param.30, bf16[4,256,1152]{2,1,0:T(8,128)(2,1)} %all-gather.8.cloned.1.call-done), kind=kOutput, calls=%fused_computation.14 | convolution fusion | flops 3623878656 | bytes 12189696 | tf_op jit(solution)/shard_map/bld,dkf->blkf/dot_general | solution.py:158
  216.0 41.2 %all-gather.10.cloned.1.call-done = bf16[4,256,1152]{2,1,0:T(8,128)(2,1)} async-done(((bf16[1,256,1152]{2,1,0:T(8,128)(2,1)}), bf16[4,256,1152]{2,1,0:T(8,128)(2,1)}) %all-gather.10.cloned.1.call-update) | async-done | bytes 2359312 | tf_op jit(solution)/shard_map/all_gather | solution.py:177
  257.2 8.4 %fusion.26 = (bf16[4,256,1,768]{3,1,0,2:T(8,128)(2,1)S(1)}, bf16[4,256,1,768]{3,1,0,2:T(8,128)(2,1)S(1)}, bf16[4,256,768]{2,1,0:T(8,128)(2,1)}) fusion(f32[4,256,2,768]{3,1,2,0:T(8,128)} %fusion.1, bf16[4,256,1152]{2,1,0:T(8,128)(2,1)} %all-gather.10.cloned.1.call-done, bf16[768,1152]{1,0:T(8,128)(2,1)} %param.31), kind=kOutput, calls=%fused_computation.62 | convolution fusion | flops 1823735808 | bytes 15138816 | tf_op jit(solution)/shard_map/bld,fd->blf/dot_general | solution.py:179
  267.3 5.6 bitcast_convert_fusion.3
  272.9 5.6 convolution_convert_fusion
  278.6 5.4 fusion.4
  284.1 1.3 convert_element_type.321
  285.4 34.1 %reduce-scatter.13.cloned.1.call-done = bf16[1,256,1152]{2,1,0:T(8,128)(2,1)} async-done(((bf16[4,256,1152]{2,1,0:T(8,128)(2,1)}), bf16[1,256,1152]{2,1,0:T(8,128)(2,1)}) %reduce-scatter.13.cloned.1.call-update) | async-done | bytes 589840 | tf_op jit(solution)/shard_map/reduce_scatter | solution.py:189
  319.5 2.6 fusion.45
  323.3 45.5 %reduce-scatter.11.cloned.1.call-done = bf16[1,256,1152]{2,1,0:T(8,128)(2,1)} async-done(((bf16[4,256,1152]{2,1,0:T(8,128)(2,1)}), bf16[1,256,1152]{2,1,0:T(8,128)(2,1)}) %reduce-scatter.11.cloned.1.call-update) | async-done | bytes 589840 | tf_op jit(solution)/shard_map/reduce_scatter | solution.py:165
  368.8 4.3 multiply_reduce_fusion.5
  374.1 1.5 convert_reduce_fusion.4
  376.4 3.0 collective-permute-start.1
  379.4 5.5 bitcast_convert_fusion
  385.0 2.1 copy.158
  387.1 6.9 collective-permute-done
  394.4 1.6 broadcast_in_dim.20
  396.8 2.1 copy.159
  398.9 5.7 collective-permute-done.1
  404.6 2.2 copy.160
  406.8 2.0 constant_dynamic-update-slice_fusion.2
  409.6 8.1 %collective-permute-done.2 = bf16[1,256,1152]{2,1,0:T(8,128)(2,1)} collective-permute-done((bf16[1,256,1152]{2,1,0:T(8,128)(2,1)}, bf16[1,256,1152]{2,1,0:T(8,128)(2,1)}, u32[]{:S(2)}, u32[]{:S(2)}) %collective-permute-start.2) | collective-permute-done | bytes 589856 | tf_op jit(solution)/shard_map/ppermute | solution.py:212
  417.7 2.1 copy.161
  419.8 2.0 constant_dynamic-update-slice_fusion
  421.8 2.9 convolution_convert_fusion.2
  425.3 2.5 multiply_reduce_fusion
  432.2 1.3 copy-done.7
  437.4 4.0 fusion.6
  441.5 2.1 fusion.47
  443.6 3.3 convolution_convert_fusion.3
  447.8 5.3 bitcast_convert_fusion.1
  453.4 6.7 bitcast_convert_fusion.2
  460.2 1.7 convert_element_type.348
  462.2 2.3 copy.177
  464.5 35.6 %reduce-scatter.19.cloned.1.call-done = bf16[288,144]{0,1:T(8,128)(2,1)} async-done(((bf16[288,1152]{0,1:T(8,128)(2,1)}), bf16[288,144]{0,1:T(8,128)(2,1)}) %reduce-scatter.19.cloned.1.call-update) | async-done | bytes 82960 | tf_op jit(solution)/shard_map/reduce_scatter | solution.py:343
  500.1 1.6 convert_element_type.344
  501.7 44.7 %reduce-scatter.17.cloned.1.call-done = bf16[144,3,288]{2,0,1:T(8,128)(2,1)} async-done(((bf16[1152,3,288]{2,0,1:T(8,128)(2,1)}), bf16[144,3,288]{2,0,1:T(8,128)(2,1)}) %reduce-scatter.17.cloned.1.call-update) | async-done | bytes 248848 | tf_op jit(solution)/shard_map/reduce_scatter | solution.py:343
  546.4 1.9 convert_element_type.335
  548.3 48.2 %reduce-scatter.15.cloned.1.call-done = bf16[1,256,1152]{2,1,0:T(8,128)(2,1)} async-done(((bf16[4,256,1152]{2,1,0:T(8,128)(2,1)}), bf16[1,256,1152]{2,1,0:T(8,128)(2,1)}) %reduce-scatter.15.cloned.1.call-update) | async-done | bytes 589840 | tf_op jit(solution)/shard_map/reduce_scatter | solution.py:267
  596.5 2.2 fusion.48
  600.6 7.7 %reduce.26 = bf16[1152,6]{1,0:T(8,128)(2,1)S(1)} reduce(bf16[1152,1,6]{2,1,0:T(2,128)(2,1)} %bitcast.210, bf16[]{:T(256)} %broadcast.439), dimensions={1}, to_apply=%bitcast.178.reduce_sub_computation | reduce | bytes 27650
  609.3 3.3 all-to-all-start.1
  613.9 2.7 fusion.38
  616.6 1.5 all-to-all-done.1
  619.4 2.8 convolution_bitcast_fusion.2
  622.2 18.0 %psum.15 = f32[4,1152]{1,0:T(4,128)S(1)} all-reduce(f32[4,1152]{1,0:T(4,128)S(1)} %convolution_bitcast_fusion.2), channel_id=1, replica_groups=mesh['dp'=8,'tensor'=4] {'tensor'}, use_global_device_ids=true, to_apply=%region_35.36 | all-reduce | flops 4608 | bytes 36864 | tf_op jit(solution)/shard_map/psum | solution.py:297
  641.1 9.2 %all-gather.1 = bf16[8,4,2880]{2,1,0:T(4,128)(2,1)S(1)} all-gather(bf16[1,4,2880]{2,1,0:T(4,128)(2,1)S(1)} %maximum_bitcast_fusion), channel_id=1, replica_groups=mesh['dp'=8,'tensor'=4] {'dp'}, dimensions={0}, use_global_device_ids=true | all-gather | bytes 207360 | tf_op jit(solution)/shard_map/all_gather | solution.py:300
  651.0 37.9 %psum.14 = f32[9360]{0:T(1024)S(1)} all-reduce(f32[9360]{0:T(1024)S(1)} %concatenate.23), channel_id=1, replica_groups=mesh['dp'=8,'tensor'=4] {'dp','tensor'}, use_global_device_ids=true, to_apply=%region_31.32 | all-reduce | flops 9360 | bytes 74880 | tf_op jit(solution)/shard_map/psum | solution.py:334
  690.3 1.9 fusion.68
  692.2 2.3 fusion.60
  696.3 1.6 convert_reduce_fusion.7
  (299 shorter events, 50.0 us)
Async XLA Ops:
  7.2 19.0 %copy-start = (bf16[1152,1152]{1,0:T(8,128)(2,1)S(1)}, bf16[1152,1152]{1,0:T(8,128)(2,1)}, u32[]{:S(2)}) copy-start(bf16[1152,1152]{1,0:T(8,128)(2,1)} %param.37) | copy-start | bytes 7962628
  21.4 6.0 copy-start.56
  21.4 6.0 copy-start.58
  24.1 3.4 copy-start.8
  27.4 6.9 copy-start.3
  29.4 10.5 %all-to-all-start = ((bf16[4,6,288]{2,1,0:T(8,128)(2,1)}), bf16[4,6,288]{2,1,0:T(8,128)(2,1)S(1)}, u32[]{:S(2)}, u32[]{:S(2)}) async-start(bf16[4,6,288]{2,1,0:T(8,128)(2,1)} %copy.149), calls=%async_computation | async-start | bytes 49152 | tf_op jit(solution)/shard_map/all_to_all | solution.py:114
  34.3 55.7 %all-gather.6.cloned.1.call-start = ((), (), s32[]{:S(2)}) async-start(), calls=%async_computation.10 | async-start | bytes 2949120 | tf_op jit(solution)/shard_map/all_gather | solution.py:122
  34.5 8.0 %copy-start.60 = (f32[256]{0:T(256)}, f32[256]{0:T(256)S(1)}, u32[]{:S(2)}) copy-start(f32[256]{0:T(256)S(1)} %broadcast_multiply_fusion.5) | copy-start | bytes 3076
  34.8 7.7 %copy-start.82 = (bf16[72]{0:T(256)(128)(2,1)S(1)}, bf16[72]{0:T(256)(128)(2,1)}, u32[]{:S(2)}) copy-start(bf16[72]{0:T(256)(128)(2,1)} %param.26) | copy-start | bytes 436
  34.8 7.7 %copy-start.83 = (bf16[72]{0:T(256)(128)(2,1)S(1)}, bf16[72]{0:T(256)(128)(2,1)}, u32[]{:S(2)}) copy-start(bf16[72]{0:T(256)(128)(2,1)} %param.27) | copy-start | bytes 436
  34.8 59.9 %copy-start.63 = (f32[256]{0:T(256)}, f32[256]{0:T(256)S(1)}, u32[]{:S(2)}) copy-start(f32[256]{0:T(256)S(1)} %add_rsqrt_fusion.1) | copy-start | bytes 3076
  42.5 110.7 %reduce-scatter.9.cloned.1.call-start = ((), (), s32[]{:S(2)}) async-start(), calls=%async_computation.11 | async-start | bytes 2949120 | tf_op jit(solution)/shard_map/reduce_scatter | solution.py:146
  42.5 52.8 %copy-start.72 = (f32[72]{0:T(128)}, f32[72]{0:T(128)S(1)}, u32[]{:S(2)}) copy-start(f32[72]{0:T(128)S(1)} %convert_element_type.306) | copy-start | bytes 868
  42.6 53.9 %copy-start.70 = (f32[72]{0:T(128)}, f32[72]{0:T(128)S(1)}, u32[]{:S(2)}) copy-start(f32[72]{0:T(128)S(1)} %convert_element_type.309) | copy-start | bytes 868
  94.7 5.9 copy-start.11
  98.2 1.6 copy-start.24
  98.2 1.6 copy-start.26
  99.8 2.0 copy-start.1
  101.9 1.7 copy-start.80
  106.5 99.9 %all-gather.8.cloned.1.call-start = ((), (), s32[]{:S(2)}) async-start(), calls=%async_computation.12 | async-start | bytes 2949120 | tf_op jit(solution)/shard_map/all_gather | solution.py:157
  153.2 2.5 copy-start.51
  153.2 2.5 copy-start.53
  156.9 100.3 %all-gather.10.cloned.1.call-start = ((), (), s32[]{:S(2)}) async-start(), calls=%async_computation.14 | async-start | bytes 2949120 | tf_op jit(solution)/shard_map/all_gather | solution.py:177
  160.3 159.2 %reduce-scatter.13.cloned.1.call-start = ((), (), s32[]{:S(2)}) async-start(), calls=%async_computation.15 | async-start | bytes 2949120 | tf_op jit(solution)/shard_map/reduce_scatter | solution.py:189
  257.2 10.1 %copy-start.77 = (bf16[1152,2,768]{2,1,0:T(2,128)(2,1)S(1)}, bf16[1152,2,768]{2,1,0:T(2,128)(2,1)}, u32[]{:S(2)}) copy-start(bf16[1152,2,768]{2,1,0:T(2,128)(2,1)} %param.30) | copy-start | bytes 10616836
  265.6 1.7 copy-start.86
  272.9 95.9 %reduce-scatter.11.cloned.1.call-start = ((), (), s32[]{:S(2)}) async-start(), calls=%async_computation.13 | async-start | bytes 2949120 | tf_op jit(solution)/shard_map/reduce_scatter | solution.py:165
  278.5 181.6 %reduce-scatter.23.cloned.1.call-start = ((), (), s32[]{:S(2)}) async-start(), calls=%async_computation.20 | async-start | bytes 1990656 | tf_op jit(solution)/shard_map/reduce_scatter | solution.py:343
  284.0 178.2 %reduce-scatter.21.cloned.1.call-start = ((), (), s32[]{:S(2)}) async-start(), calls=%async_computation.19 | async-start | bytes 3981312 | tf_op jit(solution)/shard_map/reduce_scatter | solution.py:343
  368.8 5.3 copy-start.38
  368.8 10.7 %copy-start.79 = (bf16[4,256,1152]{2,1,0:T(8,128)(2,1)S(1)}, bf16[4,256,1152]{2,1,0:T(8,128)(2,1)}, u32[]{:S(2)}) copy-start(bf16[4,256,1152]{2,1,0:T(8,128)(2,1)} %all-gather.8.cloned.1.call-done) | copy-start | bytes 7077892
  368.8 10.7 %copy-start.87 = (bf16[4,256,1,768]{3,1,0,2:T(8,128)(2,1)S(1)}, bf16[4,256,1,768]{3,1,0,2:T(8,128)(2,1)}, u32[]{:S(2)}) copy-start(bf16[4,256,1,768]{3,1,0,2:T(8,128)(2,1)} %copy-done.86) | copy-start | bytes 4718596
  373.1 6.4 copy-start.85
  375.6 18.4 %collective-permute-start = (bf16[1,256,1152]{2,1,0:T(8,128)(2,1)}, bf16[1,256,1152]{2,1,0:T(8,128)(2,1)}, u32[]{:S(2)}, u32[]{:S(2)}) collective-permute-start(bf16[1,256,1152]{2,1,0:T(8,128)(2,1)} %get-tuple-element.125), channel_id=1, source_target_pairs={{0,1},{1,2},{2,3},{3,0},{4,5},{5,6},{6,7},{7,4},{8,9},{9,10},{10,1... | collective-permute-start | bytes 1769480 | tf_op jit(solution)/shard_map/ppermute | solution.py:212
  376.4 28.2 %collective-permute-start.1 = (bf16[1,256,1152]{2,1,0:T(8,128)(2,1)}, bf16[1,256,1152]{2,1,0:T(8,128)(2,1)}, u32[]{:S(2)}, u32[]{:S(2)}) collective-permute-start(bf16[1,256,1152]{2,1,0:T(8,128)(2,1)} %get-tuple-element.125), channel_id=1, source_target_pairs={{0,3},{1,0},{2,1},{3,2},{4,7},{5,4},{6,5},{7,6},{8,11},{9,8},{10,9... | collective-permute-start | bytes 1769480 | tf_op jit(solution)/shard_map/ppermute | solution.py:221
  384.9 115.2 %reduce-scatter.19.cloned.1.call-start = ((), (), s32[]{:S(2)}) async-start(), calls=%async_computation.18 | async-start | bytes 995328 | tf_op jit(solution)/shard_map/reduce_scatter | solution.py:343
  387.1 8.9 %copy-start.16 = (bf16[1,256,1152]{1,2,0:T(8,128)(2,1)S(1)}, bf16[1,256,1152]{1,2,0:T(8,128)(2,1)}, u32[]{:S(2)}) copy-start(bf16[1,256,1152]{1,2,0:T(8,128)(2,1)} %copy.158) | copy-start | bytes 1769476
  394.0 23.7 %collective-permute-start.2 = (bf16[1,256,1152]{2,1,0:T(8,128)(2,1)}, bf16[1,256,1152]{2,1,0:T(8,128)(2,1)}, u32[]{:S(2)}, u32[]{:S(2)}) collective-permute-start(bf16[1,256,1152]{2,1,0:T(8,128)(2,1)} %collective-permute-done), channel_id=1, source_target_pairs={{0,1},{1,2},{2,3},{3,0},{4,5},{5,6},{6,7},{7,4},{8,9},{9,10},{10,1... | collective-permute-start | bytes 1769480 | tf_op jit(solution)/shard_map/ppermute | solution.py:212
  406.8 2.0 copy-start.17
  419.8 2.0 copy-start.81
  421.8 3.5 copy-start.2
  424.8 3.1 copy-start.14
  432.1 2.6 copy-start.12
  441.4 105.0 %reduce-scatter.17.cloned.1.call-start = ((), (), s32[]{:S(2)}) async-start(), calls=%async_computation.17 | async-start | bytes 2985984 | tf_op jit(solution)/shard_map/reduce_scatter | solution.py:343
  441.5 2.1 copy-start.15
  443.6 3.4 copy-start.35
  443.6 4.2 copy-start.34
  443.6 4.2 copy-start.78
  453.2 143.3 %reduce-scatter.15.cloned.1.call-start = ((), (), s32[]{:S(2)}) async-start(), calls=%async_computation.16 | async-start | bytes 2949120 | tf_op jit(solution)/shard_map/reduce_scatter | solution.py:267
  460.1 1.8 copy-start.69
  460.1 1.8 copy-start.68
  460.1 1.8 copy-start.66
  460.1 1.9 copy-start.65
  462.0 134.5 %copy-start.50 = (f32[1152]{0:T(1024)S(1)}, f32[1152]{0:T(1024)}, u32[]{:S(2)}) copy-start(f32[1152]{0:T(1024)} %copy-done.49) | copy-start | bytes 13828
  462.0 134.5 %copy-start.61 = (f32[256]{0:T(256)S(1)}, f32[256]{0:T(256)}, u32[]{:S(2)}) copy-start(f32[256]{0:T(256)} %copy-done.60) | copy-start | bytes 3076
  462.0 134.5 %copy-start.64 = (f32[256]{0:T(256)S(1)}, f32[256]{0:T(256)}, u32[]{:S(2)}) copy-start(f32[256]{0:T(256)} %copy-done.63) | copy-start | bytes 3076
  609.3 8.8 %all-to-all-start.1 = ((bf16[4,2,864]{2,1,0:T(2,128)(2,1)}), bf16[4,2,864]{2,1,0:T(2,128)(2,1)S(1)}, u32[]{:S(2)}, u32[]{:S(2)}) async-start(bf16[4,2,864]{2,1,0:T(2,128)(2,1)} %reshape.475), calls=%async_computation.6 | async-start | bytes 28672 | tf_op jit(solution)/shard_map/all_to_all | solution.py:290
  622.2 28.7 %copy-start.54 = (f32[1152]{0:T(1024)S(1)}, f32[1152]{0:T(1024)}, u32[]{:S(2)}) copy-start(f32[1152]{0:T(1024)} %get-tuple-element.122) | copy-start | bytes 13828
  622.2 28.7 %copy-start.55 = (f32[1152]{0:T(1024)S(1)}, f32[1152]{0:T(1024)}, u32[]{:S(2)}) copy-start(f32[1152]{0:T(1024)} %get-tuple-element.124) | copy-start | bytes 13828
  622.2 28.7 %copy-start.74 = (f32[72]{0:T(128)S(1)}, f32[72]{0:T(128)}, u32[]{:S(2)}) copy-start(f32[72]{0:T(128)} %get-tuple-element.104) | copy-start | bytes 868
  622.2 28.7 %copy-start.75 = (f32[72]{0:T(128)S(1)}, f32[72]{0:T(128)}, u32[]{:S(2)}) copy-start(f32[72]{0:T(128)} %get-tuple-element.102) | copy-start | bytes 868
  690.3 4.9 copy-start.76
  692.2 5.7 copy-start.57
  692.2 5.7 copy-start.59
  (40 other events, 47.2 us)
Sparse Core Ops, SparseCore 0:
  42.6 47.3 all-gather.5
  106.7 46.4 reduce-scatter.8
  157.0 49.3 all-gather.7
  208.4 48.7 all-gather.9
  273.0 46.4 reduce-scatter.12
  321.7 47.0 reduce-scatter.10
  372.1 38.6 reduce-scatter.22
  414.3 47.8 reduce-scatter.20
  465.5 34.6 reduce-scatter.18
  503.4 42.9 reduce-scatter.16
  548.7 47.7 reduce-scatter.14
